TPU v7x, 16 devices: a whole 2x2x2 slice. The times are simulated.
16 devices in a mesh: dp: 4 (over z, y), pp: 4 (over x, core).
Axes of the slice: x: 2, y: 2, z: 2, core: 2. Of those that a mesh axis runs over, the one named last changes fastest.
Arguments:
- x: bfloat16 [8, 2048, 1024], P(None, 'dp')
- t: bfloat16 [8, 2048, 1024], P(None, 'dp')
- w1: bfloat16 [4, 2, 1024, 4096], P('pp')
- w2: bfloat16 [4, 2, 4096, 1024], P('pp')
Outputs:
- output 1: float32 [4, 2, 1024, 4096], P('pp')
- output 2: float32 [4, 2, 4096, 1024], P('pp')
- output 3: float32 [], replicated
All inputs are finite; a program needn't handle non-finite values.
Results may differ from a plain program's by a relative error of at most 0.00234028.
Values are sent between devices in bfloat16 or wider.
A program may use at most 1 GiB of HBM per device.

v0:
```python
import math
import jax
import jax.numpy as jnp
from jax import lax
from jax.sharding import PartitionSpec as P


def _gelu(u):
    c = math.sqrt(2.0 / math.pi)
    return 0.5 * u * (1.0 + jnp.tanh(c * (u + 0.044715 * u * u * u)))


def _dgelu(u):
    c = math.sqrt(2.0 / math.pi)
    th = jnp.tanh(c * (u + 0.044715 * u * u * u))
    return 0.5 * (1.0 + th) + 0.5 * u * (1.0 - th * th) * c * (1.0 + 3.0 * 0.044715 * u * u)


def solution(mesh):
    ndp = mesh.shape['dp']
    npp = mesh.shape['pp']
    down = [(i, i + 1) for i in range(npp - 1)]
    up = [(i + 1, i) for i in range(npp - 1)]

    def body(x, t, w1, w2):
        nm, tok, d = x.shape
        ff = w1.shape[-1]
        w1 = w1[0]
        w2 = w2[0]
        s = lax.axis_index('pp')
        first = s == 0
        last = s == npp - 1
        inv = 1.0 / (nm * tok * ndp * d)
        nsteps = nm + npp - 1

        def fwd_step(k, c):
            recv, hbuf, ubuf, dybuf, lsum = c
            m = k - s
            valid = (m >= 0) & (m < nm)
            mc = jnp.clip(m, 0, nm - 1)
            h = jnp.where(first, x[mc], recv)
            for j in range(2):
                u = jnp.dot(h, w1[j], preferred_element_type=jnp.float32).astype(jnp.bfloat16)
                a = _gelu(u.astype(jnp.float32)).astype(jnp.bfloat16)
                hbuf = hbuf.at[j, mc].set(jnp.where(valid, h, hbuf[j, mc]))
                ubuf = ubuf.at[j, mc].set(jnp.where(valid, u, ubuf[j, mc]))
                h = (h.astype(jnp.float32) + jnp.dot(a, w2[j], preferred_element_type=jnp.float32)).astype(jnp.bfloat16)
            r = h.astype(jnp.float32) - t[mc].astype(jnp.float32)
            keep = valid & last
            lsum = lsum + jnp.where(keep, 0.5 * jnp.sum(r * r), 0.0)
            dybuf = dybuf.at[mc].set(jnp.where(keep, (r * inv).astype(jnp.bfloat16), dybuf[mc]))
            recv = lax.ppermute(h, 'pp', down)
            return recv, hbuf, ubuf, dybuf, lsum

        init = (jnp.zeros((tok, d), jnp.bfloat16),
                jnp.zeros((2, nm, tok, d), jnp.bfloat16),
                jnp.zeros((2, nm, tok, ff), jnp.bfloat16),
                jnp.zeros((nm, tok, d), jnp.bfloat16),
                jnp.zeros((), jnp.float32))
        _, hbuf, ubuf, dybuf, lsum = lax.fori_loop(0, nsteps, fwd_step, init)

        def bwd_step(k, c):
            recv, dw1, dw2 = c
            m = k - (npp - 1 - s)
            valid = (m >= 0) & (m < nm)
            mc = jnp.clip(m, 0, nm - 1)
            g = jnp.where(last, dybuf[mc], recv)
            g = jnp.where(valid, g, jnp.zeros_like(g))
            for j in (1, 0):
                h = hbuf[j, mc]
                uf = ubuf[j, mc].astype(jnp.float32)
                a = _gelu(uf).astype(jnp.bfloat16)
                q = jnp.dot(g, w2[j].T, preferred_element_type=jnp.float32)
                e = (_dgelu(uf) * q).astype(jnp.bfloat16)
                dw2 = dw2.at[j].add(jnp.dot(a.T, g, preferred_element_type=jnp.float32))
                dw1 = dw1.at[j].add(jnp.dot(h.T, e, preferred_element_type=jnp.float32))
                g = (g.astype(jnp.float32) + jnp.dot(e, w1[j].T, preferred_element_type=jnp.float32)).astype(jnp.bfloat16)
            recv = lax.ppermute(g, 'pp', up)
            return recv, dw1, dw2

        init = (jnp.zeros((tok, d), jnp.bfloat16),
                jnp.zeros((2, d, ff), jnp.float32),
                jnp.zeros((2, ff, d), jnp.float32))
        _, dw1, dw2 = lax.fori_loop(0, nsteps, bwd_step, init)
        dw1 = lax.psum(dw1, 'dp')
        dw2 = lax.psum(dw2, 'dp')
        loss = lax.psum(lsum * inv, ('dp', 'pp'))
        return dw1[None], dw2[None], loss

    return jax.shard_map(body, mesh=mesh,
                         in_specs=(P(None, 'dp', None), P(None, 'dp', None), P('pp'), P('pp')),
                         out_specs=(P('pp'), P('pp'), P()), check_vma=False)
```

profile of v0, /device:TPU:0, one launch (start us, length us, event | category | flops | bytes accessed | tf_op | source)
XLA Modules:
  0.0 3265.5 jit_solution(6073273503277520593)
XLA Ops:
  7.2 21.2 broadcast_in_dim.33
  38.9 871.8 %while.49 = (s32[]{:T(128)}, bf16[512,1024]{1,0:T(8,128)(2,1)S(1)}, bf16[2,8,512,1024]{3,2,1,0:T(8,128)(2,1)}, bf16[2,8,512,4096]{3,2,1,0:T(8,128)(2,1)}, bf16[8...) while((s32[]{:T(128)}, bf16[512,1024]{1,0:T(8,128)(2,1)S(1)}, ...), condition=%wide.region_5.6_spmd, body=%wide.region_0.5_spmd.sunk | while | flops 17246453760 | bytes 130029520 | solution.py:60
  933.8 1150.6 %while.50 = (s32[]{:T(128)}, bf16[512,1024]{1,0:T(8,128)(2,1)S(1)}, f32[2,1024,4096]{2,1,0:T(8,128)}, f32[2,4096,1024]{2,1,0:T(8,128)}, s32[]{:T(128)}, /*index=...) while((s32[]{:T(128)}, bf16[512,1024]{1,0:T(8,128)(2,1)S(1)}, ...), condition=%wide.region_7.8_spmd, body=%wide.region_6.7_spmd.sunk | while | flops 34506539008 | bytes 277872992 | solution.py:84
  996.1 14.2 fusion.207
  1010.3 14.3 fusion.208
  1024.6 18.2 fusion.205
  1099.0 14.2 fusion.207
  1113.2 14.3 fusion.208
  1127.5 18.2 fusion.205
  1216.2 14.3 fusion.208
  1230.4 18.2 fusion.205
  1304.9 14.2 fusion.207
  1319.1 14.3 fusion.208
  1333.4 18.2 fusion.205
  1422.0 14.3 fusion.208
  1436.3 18.2 fusion.205
  1510.8 14.2 fusion.207
  1525.0 14.3 fusion.208
  1539.3 18.2 fusion.205
  1627.9 14.3 fusion.208
  1642.2 18.2 fusion.205
  1730.9 14.3 fusion.208
  1745.1 18.2 fusion.205
  1833.8 14.3 fusion.208
  1848.1 18.2 fusion.205
  1936.7 14.3 fusion.208
  1951.0 18.2 fusion.205
  2039.7 14.3 fusion.208
  2053.9 18.2 fusion.205
  2084.4 52.7 %psum.23 = f32[]{:T(128)} all-reduce(f32[]{:T(128)S(6)} %mul.398), channel_id=1, replica_groups=mesh['dp'=4,'pp'=4] {'dp','pp'}, use_global_device_ids=true, to_apply=%region_10.11 | all-reduce | flops 1 | bytes 8 | tf_op jit(solution)/shard_map/psum | solution.py:87
  2137.1 1077.7 %all-reduce.3.cloned.1.call-done = (f32[1,2,1024,4096]{3,2,1,0:T(8,128)}, f32[1,2,4096,1024]{3,2,1,0:T(8,128)}) async-done(((f32[1,2,1024,4096]{3,2,1,0:T(8,128)}, f32[1,2,4096,1024]{3,2,1,0:T(8,128)}), (f32[1,2,1024,4096]{3,2,1,0:T(8,128)}, f32[1,2,4096,1024]{3,2,1,0:T(8,128)})) %all-reduce.3.cloned.1.call-update) | async-done | bytes 67108880 | tf_op jit(solution)/shard_map/psum | solution.py:85
  3214.8 24.3 copy.48
  (363 shorter events, 1633.8 us)
Async XLA Ops:
  7.2 3207.6 %all-reduce.3.cloned.1.call-start = ((), (), s32[]{:S(2)}) async-start(), calls=%async_computation | async-start | bytes 134217728 | tf_op jit(solution)/shard_map/psum | solution.py:85
  103.1 5.8 collective-permute-start
  173.0 16.2 collective-permute-start
  253.2 16.1 collective-permute-start
  333.4 16.1 collective-permute-start
  413.7 16.0 collective-permute-start
  493.8 16.1 collective-permute-start
  574.0 16.0 collective-permute-start
  654.1 16.0 collective-permute-start
  734.3 16.1 collective-permute-start
  814.5 16.0 collective-permute-start
  894.7 16.1 collective-permute-start
  994.8 60.2 %collective-permute-start.1 = (bf16[512,1024]{1,0:T(8,128)(2,1)S(1)}, bf16[512,1024]{1,0:T(8,128)(2,1)S(1)}, u32[]{:S(2)}, u32[]{:S(2)}) collective-permute-start(bf16[512,1024]{1,0:T(8,128)(2,1)S(1)} %add_convert_fusion.7), channel_id=1, source_target_pairs={{1,0},{2,1},{3,2},{5,4},{6,5},{7,6},{9,8},{10,9},{11,10},{13,12},{... | collective-permute-start | bytes 3145736 | tf_op jit(solution)/shard_map/while/body/eval_jaxpr/ppermute | solution.py:78
  1024.6 18.2 copy-start.1
  1097.7 60.2 %collective-permute-start.1 = (bf16[512,1024]{1,0:T(8,128)(2,1)S(1)}, bf16[512,1024]{1,0:T(8,128)(2,1)S(1)}, u32[]{:S(2)}, u32[]{:S(2)}) collective-permute-start(bf16[512,1024]{1,0:T(8,128)(2,1)S(1)} %add_convert_fusion.7), channel_id=1, source_target_pairs={{1,0},{2,1},{3,2},{5,4},{6,5},{7,6},{9,8},{10,9},{11,10},{13,12},{... | collective-permute-start | bytes 3145736 | tf_op jit(solution)/shard_map/while/body/eval_jaxpr/ppermute | solution.py:78
  1127.5 18.2 copy-start.1
  1200.7 60.2 %collective-permute-start.1 = (bf16[512,1024]{1,0:T(8,128)(2,1)S(1)}, bf16[512,1024]{1,0:T(8,128)(2,1)S(1)}, u32[]{:S(2)}, u32[]{:S(2)}) collective-permute-start(bf16[512,1024]{1,0:T(8,128)(2,1)S(1)} %add_convert_fusion.7), channel_id=1, source_target_pairs={{1,0},{2,1},{3,2},{5,4},{6,5},{7,6},{9,8},{10,9},{11,10},{13,12},{... | collective-permute-start | bytes 3145736 | tf_op jit(solution)/shard_map/while/body/eval_jaxpr/ppermute | solution.py:78
  1230.4 18.2 copy-start.1
  1303.6 60.2 %collective-permute-start.1 = (bf16[512,1024]{1,0:T(8,128)(2,1)S(1)}, bf16[512,1024]{1,0:T(8,128)(2,1)S(1)}, u32[]{:S(2)}, u32[]{:S(2)}) collective-permute-start(bf16[512,1024]{1,0:T(8,128)(2,1)S(1)} %add_convert_fusion.7), channel_id=1, source_target_pairs={{1,0},{2,1},{3,2},{5,4},{6,5},{7,6},{9,8},{10,9},{11,10},{13,12},{... | collective-permute-start | bytes 3145736 | tf_op jit(solution)/shard_map/while/body/eval_jaxpr/ppermute | solution.py:78
  1333.4 18.2 copy-start.1
  1406.5 60.2 %collective-permute-start.1 = (bf16[512,1024]{1,0:T(8,128)(2,1)S(1)}, bf16[512,1024]{1,0:T(8,128)(2,1)S(1)}, u32[]{:S(2)}, u32[]{:S(2)}) collective-permute-start(bf16[512,1024]{1,0:T(8,128)(2,1)S(1)} %add_convert_fusion.7), channel_id=1, source_target_pairs={{1,0},{2,1},{3,2},{5,4},{6,5},{7,6},{9,8},{10,9},{11,10},{13,12},{... | collective-permute-start | bytes 3145736 | tf_op jit(solution)/shard_map/while/body/eval_jaxpr/ppermute | solution.py:78
  1436.3 18.2 copy-start.1
  1509.5 60.2 %collective-permute-start.1 = (bf16[512,1024]{1,0:T(8,128)(2,1)S(1)}, bf16[512,1024]{1,0:T(8,128)(2,1)S(1)}, u32[]{:S(2)}, u32[]{:S(2)}) collective-permute-start(bf16[512,1024]{1,0:T(8,128)(2,1)S(1)} %add_convert_fusion.7), channel_id=1, source_target_pairs={{1,0},{2,1},{3,2},{5,4},{6,5},{7,6},{9,8},{10,9},{11,10},{13,12},{... | collective-permute-start | bytes 3145736 | tf_op jit(solution)/shard_map/while/body/eval_jaxpr/ppermute | solution.py:78
  1539.3 18.2 copy-start.1
  1612.4 60.2 %collective-permute-start.1 = (bf16[512,1024]{1,0:T(8,128)(2,1)S(1)}, bf16[512,1024]{1,0:T(8,128)(2,1)S(1)}, u32[]{:S(2)}, u32[]{:S(2)}) collective-permute-start(bf16[512,1024]{1,0:T(8,128)(2,1)S(1)} %add_convert_fusion.7), channel_id=1, source_target_pairs={{1,0},{2,1},{3,2},{5,4},{6,5},{7,6},{9,8},{10,9},{11,10},{13,12},{... | collective-permute-start | bytes 3145736 | tf_op jit(solution)/shard_map/while/body/eval_jaxpr/ppermute | solution.py:78
  1642.2 18.2 copy-start.1
  1715.4 60.2 %collective-permute-start.1 = (bf16[512,1024]{1,0:T(8,128)(2,1)S(1)}, bf16[512,1024]{1,0:T(8,128)(2,1)S(1)}, u32[]{:S(2)}, u32[]{:S(2)}) collective-permute-start(bf16[512,1024]{1,0:T(8,128)(2,1)S(1)} %add_convert_fusion.7), channel_id=1, source_target_pairs={{1,0},{2,1},{3,2},{5,4},{6,5},{7,6},{9,8},{10,9},{11,10},{13,12},{... | collective-permute-start | bytes 3145736 | tf_op jit(solution)/shard_map/while/body/eval_jaxpr/ppermute | solution.py:78
  1745.1 18.2 copy-start.1
  1818.3 60.2 %collective-permute-start.1 = (bf16[512,1024]{1,0:T(8,128)(2,1)S(1)}, bf16[512,1024]{1,0:T(8,128)(2,1)S(1)}, u32[]{:S(2)}, u32[]{:S(2)}) collective-permute-start(bf16[512,1024]{1,0:T(8,128)(2,1)S(1)} %add_convert_fusion.7), channel_id=1, source_target_pairs={{1,0},{2,1},{3,2},{5,4},{6,5},{7,6},{9,8},{10,9},{11,10},{13,12},{... | collective-permute-start | bytes 3145736 | tf_op jit(solution)/shard_map/while/body/eval_jaxpr/ppermute | solution.py:78
  1921.2 60.2 %collective-permute-start.1 = (bf16[512,1024]{1,0:T(8,128)(2,1)S(1)}, bf16[512,1024]{1,0:T(8,128)(2,1)S(1)}, u32[]{:S(2)}, u32[]{:S(2)}) collective-permute-start(bf16[512,1024]{1,0:T(8,128)(2,1)S(1)} %add_convert_fusion.7), channel_id=1, source_target_pairs={{1,0},{2,1},{3,2},{5,4},{6,5},{7,6},{9,8},{10,9},{11,10},{13,12},{... | collective-permute-start | bytes 3145736 | tf_op jit(solution)/shard_map/while/body/eval_jaxpr/ppermute | solution.py:78
  2024.2 60.2 %collective-permute-start.1 = (bf16[512,1024]{1,0:T(8,128)(2,1)S(1)}, bf16[512,1024]{1,0:T(8,128)(2,1)S(1)}, u32[]{:S(2)}, u32[]{:S(2)}) collective-permute-start(bf16[512,1024]{1,0:T(8,128)(2,1)S(1)} %add_convert_fusion.7), channel_id=1, source_target_pairs={{1,0},{2,1},{3,2},{5,4},{6,5},{7,6},{9,8},{10,9},{11,10},{13,12},{... | collective-permute-start | bytes 3145736 | tf_op jit(solution)/shard_map/while/body/eval_jaxpr/ppermute | solution.py:78
  3214.8 31.8 copy-start.4
  (38 other events, 315.2 us)
Sparse Core Ops, SparseCore 0:
  2084.5 1130.2 all-reduce.2
where the time goes:
time: 3280 us; the launch traced here: 3270 us
  matrix products  1580 us (48%)
  waiting for transfers between devices  1080 us (33%)
  local copies, waits for them, and re-layouts  266 us (8%)
  starting transfers between devices  147 us (4%)
  other arithmetic  96.7 us (3%)
  blocking collectives  52.7 us (2%)
    psum x1, waiting for transfers between devices, body(): dw1 = lax.psum(dw1, 'dp')  1080 us
    dot_general x22, matrix products, bwd_step(): dw1 = dw1.at[j].add(jnp.dot(h.T, e, preferred_element_type=jnp.float32))  335 us
    dot_general x22, matrix products, bwd_step(): dw2 = dw2.at[j].add(jnp.dot(a.T, g, preferred_element_type=jnp.float32))  313 us
    dot_general x22, matrix products, bwd_step(): q = jnp.dot(g, w2[j].T, preferred_element_type=jnp.float32)  258 us
    dot_general x22, matrix products, fwd_step(): jnp.dot(a, w2[j], preferred_element_type=jnp.float32)  255 us
    dot_general x22, matrix products, fwd_step(): jnp.dot(h, w1[j], preferred_element_type=jnp.float32).astype(jnp.bfloat16)  248 us
    dot_general x22, matrix products, bwd_step(): jnp.dot(e, w1[j].T, preferred_element_type=jnp.float32)  175 us
    ppermute x11, starting transfers between devices, fwd_step(): recv = lax.ppermute(h, 'pp', down)  133 us
  transfers between devices with their start and end apart: 23, of which 1 were waited for; matrix products, arithmetic and copies ran while one was open for 21% of the time, Pallas kernels for 0%

commit v1 on v0

v1 whole, which is shorter than its diff:
```python
import functools
import math

import jax
import jax.numpy as jnp
from jax import lax
from jax.experimental import pallas as pl
from jax.experimental.pallas import tpu as pltpu
from jax.sharding import PartitionSpec as P

MESH = pl.DeviceIdType.MESH
F32 = jnp.float32
BF16 = jnp.bfloat16
VMEM_LIMIT = 67_043_328
C0 = math.sqrt(2.0 / math.pi)
C1 = 0.044715

D = 1024
FF = 4096
R = 256
NK = 16
FC = 512
TOK = R * NK

BC = 256
NB = FF // BC
HB = BC // 2
TC = 1024
NQ = 2 * TOK // TC

NT = (((1,), (1,)), ((), ()))


def _dot(a, b):
    return jnp.dot(a, b, preferred_element_type=F32)


def _dot_t(a, b):
    return lax.dot_general(a, b, NT, preferred_element_type=F32)


def _act(u):
    t2 = u * u
    th = jnp.tanh(u * (C0 + (C0 * C1) * t2))
    return th, 0.5 * u, t2


def _gelu(u):
    th, hu, _ = _act(u)
    return hu + hu * th


def _dgelu(th, hu, t2):
    return (0.5 + 0.5 * th) + (hu * (1.0 - th * th)) * (C0 + (3.0 * C0 * C1) * t2)


def _pipe_kernel(inv, x, t, w1, w2, hl, gl, wl1, wl2, us, lo,
                 W1, W2, hin, gin, ub, ab, hgb, hop, tb,
                 sw, sx, sg, st, su, sh0, sg2, shg, sop, lh, lg, swl, rwl):
    e = lax.axis_index('dp')
    s = lax.axis_index('pp')
    c = s % 2
    xx = s // 2
    slot = e % 2
    tcore = 2 * xx + e // 2
    first = s == 0
    last = s == 3

    def wcopy(j, i):
        if i == 0:
            return pltpu.make_async_copy(w1.at[j], W1.at[j], sw.at[2 * j])
        return pltpu.make_async_copy(w2.at[j], W2.at[j], sw.at[2 * j + 1])

    for j in range(2):
        for i in range(2):
            wcopy(j, i).start()

    def xcopy(k):
        return pltpu.make_async_copy(x.at[k // 2, pl.ds(pl.multiple_of((k % 2) * R, R), R)], hin.at[k], sx.at[k])

    @pl.when(first)
    def _():
        lax.fori_loop(0, NK, lambda k, z: (xcopy(k).start(), z)[1], 0)

    def wl_copy(i):
        src, dst = ((w1, wl1), (w2, wl2))[i]
        return pltpu.make_async_remote_copy(src.at[e % 2], dst, swl.at[i], rwl.at[i],
                                            device_id=(e, 2 * xx + 1 - c), device_id_type=MESH)

    @pl.when(c == e // 2)
    def _():
        for i in range(2):
            wl_copy(i).start()

    lo[...] = jnp.zeros_like(lo)

    def rows(k):
        return pl.ds(pl.multiple_of(k * R, R), R)

    def ship(src, dst, k, j, sem, land):
        d = 2 * c + j

        @pl.when(d == e)
        def _():
            pltpu.make_async_copy(src, dst.at[slot, rows(k)], sem).start()

        @pl.when(d != e)
        def _():
            pltpu.make_async_remote_copy(src, dst.at[slot, rows(k)], sem, land.at[slot],
                                         device_id=(d, tcore), device_id_type=MESH).start()

    def tile_wait(buf, sem):
        pltpu.make_async_copy(buf, hl.at[0, pl.ds(0, R)], sem).wait()

    def fwd(k, z):
        h4 = k % 4
        h2 = k % 2
        pltpu.make_async_copy(hl.at[0, pl.ds(0, R)], hin.at[k], sx.at[k]).wait()
        ship(hin.at[k], hl, k, 0, sh0, lh)

        @pl.when(last)
        def _():
            pltpu.make_async_copy(t.at[k // 2, pl.ds(pl.multiple_of((k % 2) * R, R), R)], tb, st).start()

        def layer(h, j):
            @pl.when(k == 0)
            def _():
                wcopy(j, 0).wait()
                wcopy(j, 1).wait()

            @pl.when(k > 0)
            def _():
                pltpu.make_async_copy(ub.at[j], us.at[j, k - 1], su.at[j]).wait()

            for f in range(FF // FC):
                cs = slice(f * FC, (f + 1) * FC)
                u = _dot(h, W1[j, :, cs]).astype(BF16)
                ub[j, :, cs] = u
                ab[:, cs] = _gelu(u.astype(F32)).astype(BF16)
            acc = _dot(ab[...], W2[j])
            out = (h.astype(F32) + acc).astype(BF16)
            pltpu.make_async_copy(ub.at[j], us.at[j, k], su.at[j]).start()
            return out

        h1 = layer(hin[k], 0)

        @pl.when(k >= 4)
        def _():
            tile_wait(hgb.at[h4], shg.at[h4])
        hgb[h4] = h1
        y = layer(hgb[h4], 1)
        ship(hgb.at[h4], hl, k, 1, shg.at[h4], lh)

        @pl.when(jnp.logical_and(k >= 2, s < 3))
        def _():
            tile_wait(hop.at[h2], sop.at[h2])
        hop[h2] = y

        @pl.when(s < 3)
        def _():
            pltpu.make_async_remote_copy(hop.at[h2], hin.at[k], sop.at[h2], sx.at[k],
                                         device_id=(e, s + 1), device_id_type=MESH).start()

        @pl.when(last)
        def _():
            pltpu.make_async_copy(t.at[0, pl.ds(0, R)], tb, st).wait()
            r = hop[h2].astype(F32) - tb[...].astype(F32)
            lo[...] += jnp.sum((r * r).reshape(R // 8, 8, D), axis=0)
            gin[k] = (r * inv).astype(BF16)
        return z

    lax.fori_loop(0, NK, fwd, 0)

    for j in range(2):
        pltpu.make_async_copy(ub.at[j], us.at[j, NK - 1], su.at[j]).wait()
        pltpu.make_async_copy(us.at[j, 0], ub.at[j], su.at[j]).start()

    def bwd(k, z):
        h4 = k % 4
        h2 = k % 2

        @pl.when(s < 3)
        def _():
            pltpu.make_async_copy(hl.at[0, pl.ds(0, R)], gin.at[k], sg.at[k]).wait()
        ship(gin.at[k], gl, k, 1, sg2, lg)

        def layer(g, j):
            pltpu.make_async_copy(us.at[j, k], ub.at[j], su.at[j]).wait()
            for f in range(FF // FC):
                cs = slice(f * FC, (f + 1) * FC)
                q = _dot_t(g, W2[j, cs, :])
                th, hu, t2 = _act(ub[j, :, cs].astype(F32))
                ab[:, cs] = (_dgelu(th, hu, t2) * q).astype(BF16)
            acc = _dot_t(ab[...], W1[j])
            out = (g.astype(F32) + acc).astype(BF16)

            @pl.when(k < NK - 1)
            def _():
                pltpu.make_async_copy(us.at[j, k + 1], ub.at[j], su.at[j]).start()
            return out

        g1 = layer(gin[k], 1)
        tile_wait(hgb.at[h4], shg.at[h4])
        hgb[h4] = g1

        @pl.when(s > 0)
        def _():
            g0 = layer(hgb[h4], 0)

            @pl.when(jnp.logical_or(k >= 2, s < 3))
            def _():
                tile_wait(hop.at[h2], sop.at[h2])
            hop[h2] = g0
            pltpu.make_async_remote_copy(hop.at[h2], gin.at[k], sop.at[h2], sg.at[k],
                                         device_id=(e, s - 1), device_id_type=MESH).start()
        ship(hgb.at[h4], gl, k, 0, shg.at[h4], lg)
        return z

    lax.fori_loop(0, NK, bwd, 0)

    @pl.when(s == 0)
    def _():
        pltpu.make_async_copy(us.at[0, 0], ub.at[0], su.at[0]).wait()
    for i in range(4):
        tile_wait(hgb.at[i], shg.at[i])
    for i in range(2):
        tile_wait(hop.at[i], sop.at[i])
    pltpu.make_async_copy(hl.at[0], gl.at[0], sh0).wait()
    pltpu.make_async_copy(hl.at[0], gl.at[0], sg2).wait()
    for i in range(2):
        @pl.when(2 * c + i != e)
        def _():
            pltpu.make_async_copy(hl.at[i], gl.at[i], lh.at[i]).wait()
            pltpu.make_async_copy(hl.at[i], gl.at[i], lg.at[i]).wait()

    @pl.when(c == e // 2)
    def _():
        for i in range(2):
            wl_copy(i).wait_send()

    @pl.when(c != e // 2)
    def _():
        for i in range(2):
            wl_copy(i).wait_recv()


def _pipe(x, t, w1, w2, inv):
    hbm = pl.BlockSpec(memory_space=pl.ANY)
    dma = pltpu.SemaphoreType.DMA
    return pl.pallas_call(
        functools.partial(_pipe_kernel, inv),
        name="pipe",
        out_shape=(
            jax.ShapeDtypeStruct((2, TOK, D), BF16),
            jax.ShapeDtypeStruct((2, TOK, D), BF16),
            jax.ShapeDtypeStruct((D, FF), BF16),
            jax.ShapeDtypeStruct((FF, D), BF16),
            jax.ShapeDtypeStruct((2, NK, R, FF), BF16),
            jax.ShapeDtypeStruct((8, D), F32),
        ),
        in_specs=[hbm] * 4,
        out_specs=(hbm,) * 5 + (pl.BlockSpec(memory_space=pltpu.VMEM),),
        scratch_shapes=[
            pltpu.VMEM((2, D, FF), BF16),
            pltpu.VMEM((2, FF, D), BF16),
            pltpu.VMEM((NK, R, D), BF16),
            pltpu.VMEM((NK, R, D), BF16),
            pltpu.VMEM((2, R, FF), BF16),
            pltpu.VMEM((R, FF), BF16),
            pltpu.VMEM((4, R, D), BF16),
            pltpu.VMEM((2, R, D), BF16),
            pltpu.VMEM((R, D), BF16),
            dma((4,)), dma((NK,)), dma((NK,)), dma, dma((2,)), dma, dma,
            dma((4,)), dma((2,)), dma((2,)), dma((2,)), dma((2,)), dma((2,)),
        ],
        compiler_params=pltpu.CompilerParams(has_side_effects=True, vmem_limit_bytes=VMEM_LIMIT),
    )(x, t, w1, w2)


def _grad_kernel(hl, gl, w1, w2, wl1, wl2, o1, o2,
                 hres, gres, wb1, wb2, wt, p1, p2, r1, r2, f1, f2,
                 slh, slg, swb, sxs, sxr, ssl, sscw, ssccw, rab, rc, rd, sf):
    d = lax.axis_index('dp')
    s = lax.axis_index('pp')
    c = s % 2
    xx = s // 2
    t = d // 2
    j = d % 2
    zz = d // 2
    yy = d % 2
    nxt = 2 * yy + 1 - zz
    prv = 2 * (1 - yy) + zz
    tgt = 2 * xx + t
    partner = 2 * xx + 1 - c

    def load(q):
        src = (q % 2, pl.ds(pl.multiple_of((q // 2) * TC, TC), TC))
        dst = (pl.ds(pl.multiple_of(q * TC, TC), TC),)
        return (pltpu.make_async_copy(hl.at[src], hres.at[dst], slh.at[q]),
                pltpu.make_async_copy(gl.at[src], gres.at[dst], slg.at[q]))

    def wload_start(b):
        sl = b % 2
        cs = pl.ds(pl.multiple_of(b * BC, BC), BC)

        @pl.when(c == t)
        def _():
            pltpu.make_async_copy(w1.at[j, :, cs], wb1.at[sl], swb.at[sl, 0]).start()
            pltpu.make_async_copy(w2.at[j, cs, :], wb2.at[sl], swb.at[sl, 1]).start()

        @pl.when(c != t)
        def _():
            pltpu.make_async_copy(wl1.at[:, cs], wb1.at[sl], swb.at[sl, 0]).start()
            pltpu.make_async_copy(wl2.at[cs, :], wb2.at[sl], swb.at[sl, 1]).start()

    def wload_wait(b):
        sl = b % 2
        pltpu.make_async_copy(wl1.at[:, pl.ds(0, BC)], wb1.at[sl], swb.at[sl, 0]).wait()
        pltpu.make_async_copy(wl2.at[pl.ds(0, BC), :], wb2.at[sl], swb.at[sl, 1]).wait()

    wload_start(0)
    for q in range(NQ):
        for cp in load(q):
            cp.start()

    mine = pl.ds(pl.multiple_of(c * HB, HB), HB)
    theirs = pl.ds(pl.multiple_of((1 - c) * HB, HB), HB)

    def exchange(b):
        sl = b % 2
        return [pltpu.make_async_remote_copy(p.at[sl, theirs, :], r.at[sl], sxs.at[sl, i], sxr.at[sl, i],
                                             device_id=(d, partner), device_id_type=MESH)
                for i, (p, r) in enumerate(((p1, r1), (p2, r2)))]

    def region(i, jj, b, half):
        cs = pl.ds(pl.multiple_of(b * BC + half * HB, HB), HB)
        return o1.at[jj, :, cs] if i == 0 else o2.at[jj, cs, :]

    def finish(b):
        sl = b % 2
        for cp in exchange(b):
            cp.wait()
        f1[b] = (p1[sl, mine, :] + r1[sl]).T
        f2[b] = p2[sl, mine, :] + r2[sl]
        for i, f in enumerate((f1, f2)):
            dst = region(i, j, b, c)
            pltpu.make_async_remote_copy(f.at[b], dst, sscw.at[i], rab.at[c, i, b],
                                         device_id=(nxt, tgt), device_id_type=MESH).start()
            pltpu.make_async_remote_copy(f.at[b], dst, ssccw.at[i], rab.at[1 - c, i, b],
                                         device_id=(prv, tgt), device_id_type=MESH).start()

            @pl.when(c == t)
            def _():
                pltpu.make_async_copy(f.at[b], dst, ssl.at[i]).start()

            @pl.when(c != t)
            def _():
                pltpu.make_async_remote_copy(f.at[b], dst, ssl.at[i], rd.at[i],
                                             device_id=(d, tgt), device_id_type=MESH).start()

    def block(b, z):
        sl = b % 2
        wload_wait(b)
        wt[...] = wb1[sl].T
        p1[sl] = jnp.zeros((BC, D), F32)
        p2[sl] = jnp.zeros((BC, D), F32)

        @pl.when(b < NB - 1)
        def _():
            wload_start(b + 1)

        def chunk(q, z2):
            @pl.when(b == 0)
            def _():
                for cp in load(q):
                    cp.wait()

            rs = pl.ds(pl.multiple_of(q * TC, TC), TC)
            ut = _dot_t(wt[...], hres[rs, :])
            qt = _dot_t(wb2[sl], gres[rs, :])
            th, hu, t2 = _act(ut.astype(BF16).astype(F32))
            a = (hu + hu * th).astype(BF16)
            ee = (_dgelu(th, hu, t2) * qt).astype(BF16)
            p1[sl] += _dot(ee, hres[rs, :])
            p2[sl] += _dot(a, gres[rs, :])

            @pl.when(jnp.logical_and(q == 0, b > 0))
            def _():
                finish(b - 1)
            return z2

        lax.fori_loop(0, NQ, chunk, 0)
        for cp in exchange(b):
            cp.start()
        return z

    lax.fori_loop(0, NB, block, 0)
    finish(NB - 1)

    cw = prv // 2 == c
    src_chip = jnp.where(cw, prv, nxt)
    half = jnp.where(cw, 0, 1)
    onward = jnp.where(cw, nxt, prv)

    def forward(b, z):
        for i in range(2):
            reg = region(i, src_chip % 2, b, half)
            cp = pltpu.make_async_remote_copy(reg, reg, sf.at[i], rab.at[0, i, b],
                                              device_id=(onward, s), device_id_type=MESH)
            cp.wait_recv()
            pltpu.make_async_remote_copy(reg, reg, sf.at[i], rc.at[half, i],
                                         device_id=(onward, s), device_id_type=MESH).start()
        return z

    lax.fori_loop(0, NB, forward, 0)

    def others(b, z):
        for i in range(2):
            reg = region(i, src_chip % 2, b, 1 - half)
            pltpu.make_async_remote_copy(reg, reg, sf.at[i], rab.at[1, i, b],
                                         device_id=(onward, s), device_id_type=MESH).wait_recv()
        return z

    lax.fori_loop(0, NB, others, 0)

    for i, f in enumerate((f1, f2)):
        big = o1.at[0, :, pl.ds(0, FF // 2)] if i == 0 else o2.at[0, pl.ds(0, FF // 2), :]
        for sem in (sscw, ssccw, ssl):
            pltpu.make_async_copy(big, big, sem.at[i]).wait()
        pltpu.make_async_copy(big, big, sf.at[i]).wait()

        @pl.when(c == t)
        def _():
            pltpu.make_async_copy(big, big, rd.at[i]).wait()

        @pl.when(c != t)
        def _():
            pltpu.make_async_copy(big, big, rc.at[0, i]).wait()
            pltpu.make_async_copy(big, big, rc.at[1, i]).wait()


def _grads(hl, gl, w1, w2, wl1, wl2):
    hbm = pl.BlockSpec(memory_space=pl.ANY)
    dma = pltpu.SemaphoreType.DMA
    return pl.pallas_call(
        _grad_kernel,
        name="grads",
        out_shape=(jax.ShapeDtypeStruct((2, D, FF), F32), jax.ShapeDtypeStruct((2, FF, D), F32)),
        in_specs=[hbm] * 6,
        out_specs=(hbm, hbm),
        scratch_shapes=[
            pltpu.VMEM((2 * TOK, D), BF16),
            pltpu.VMEM((2 * TOK, D), BF16),
            pltpu.VMEM((2, D, BC), BF16),
            pltpu.VMEM((2, BC, D), BF16),
            pltpu.VMEM((BC, D), BF16),
            pltpu.VMEM((2, BC, D), F32),
            pltpu.VMEM((2, BC, D), F32),
            pltpu.VMEM((2, HB, D), F32),
            pltpu.VMEM((2, HB, D), F32),
            pltpu.VMEM((NB, D, HB), F32),
            pltpu.VMEM((NB, HB, D), F32),
            dma((NQ,)), dma((NQ,)), dma((2, 2)), dma((2, 2)), dma((2, 2)),
            dma((2,)), dma((2,)), dma((2,)), dma((2, 2, NB)), dma((2, 2)), dma((2,)), dma((2,)),
        ],
        compiler_params=pltpu.CompilerParams(has_side_effects=True, vmem_limit_bytes=VMEM_LIMIT),
    )(hl, gl, w1, w2, wl1, wl2)


def solution(mesh):
    ndp = mesh.shape['dp']

    def body(x, t, w1, w2):
        nm, tok, d = x.shape
        inv = 1.0 / (nm * tok * ndp * d)
        hl, gl, wl1, wl2, _, lo = _pipe(x, t, w1[0], w2[0], inv)
        dw1, dw2 = _grads(hl, gl, w1[0], w2[0], wl1, wl2)
        loss = lax.psum(jnp.sum(lo) * (0.5 * inv), ('dp', 'pp'))
        return dw1[None], dw2[None], loss

    return jax.shard_map(body, mesh=mesh,
                         in_specs=(P(None, 'dp', None), P(None, 'dp', None), P('pp'), P('pp')),
                         out_specs=(P('pp'), P('pp'), P()), check_vma=False)
```

time: 3280 us -> 1140 us (0.35)
  matrix products: 1580 us -> 0 us
  waiting for transfers between devices: 1080 us -> 0 us
  Pallas kernels: 0 us -> 1060 us
  local copies, waits for them, and re-layouts: 266 us -> 43.5 us
  starting transfers between devices: 147 us -> 0 us
  other arithmetic: 96.7 us -> 1.37 us
    dot_general x132 -> x0, matrix products: 1580 us -> none  [the longest x22 335 us: bwd_step(): dw1 = dw1.at[j].add(jnp.dot(h.T, e, preferred_element_type=jnp.float32))]
    psum x1 -> x0, waiting for transfers between devices: 1080 us -> none  [body(): dw1 = lax.psum(dw1, 'dp')]
    pallas_call x0 -> x2, Pallas kernels: none -> 1060 us  [the longest x1 578 us: _grads(): pl.pallas_call(_grad_kernel, name='grads', out_shape=(jax.ShapeDtypeStruc...]
    ppermute x22 -> x0, starting transfers between devices: 147 us -> none  [the longest x11 133 us: fwd_step(): recv = lax.ppermute(h, 'pp', down)]
    dynamic_slice x55 -> x0, local copies, waits for them, and re-layouts: 146 us -> none  [the longest x22 103 us: fwd_step(): ubuf = ubuf.at[j, mc].set(jnp.where(valid, u, ubuf[j, mc]))]
    broadcast_in_dim x5 -> x0, local copies, waits for them, and re-layouts: 54.5 us -> none  [the longest x1 21.2 us: body(): jnp.zeros((2, nm, tok, ff), jnp.bfloat16)]
    scatter x11 -> x0, other arithmetic: 40 us -> none  [fwd_step(): hbuf = hbuf.at[j, mc].set(jnp.where(valid, h, hbuf[j, mc]))]
  transfers between devices with their start and end apart: 23 -> 0, of which waited for: 1 -> 0; matrix products, arithmetic and copies ran while one was open for 21% -> 0% of each run, Pallas kernels for 0% -> 0%
where the time goes in v1:
time: 1140 us
  Pallas kernels  1060 us (93%)
  local copies, waits for them, and re-layouts  43.5 us (4%)
  blocking collectives  33.1 us (3%)
    pallas_call x1, Pallas kernels, _grads(): pl.pallas_call(_grad_kernel, name='grads', out_shape=(jax.ShapeDtypeStruc...  578 us
    pallas_call x1, Pallas kernels, _pipe(): pl.pallas_call(functools.partial(_pipe_kernel, inv), name='pipe', out_sha...  480 us
    unnamed x18, local copies, waits for them, and re-layouts  43.5 us
    psum x1, blocking collectives, body(): loss = lax.psum(jnp.sum(lo) * (0.5 * inv), ('dp', 'pp'))  33.1 us

profile of v1, /device:TPU:0, one launch (start us, length us, event | category | flops | bytes accessed | tf_op | source)
XLA Modules:
  0.0 1137.2 jit_solution(1699681347224561959)
XLA Ops:
  0.6 480.4 %pipe.1 = (bf16[2,4096,1024]{2,1,0:T(8,128)(2,1)}, bf16[2,4096,1024]{2,1,0:T(8,128)(2,1)}, bf16[1024,4096]{1,0:T(8,128)(2,1)}, bf16[4096,1024]{1,0:T(8,128)(2,1)...) custom-call(bf16[8,512,1024]{2,1,0:T(8,128)(2,1)} %x.1, bf16[8,512,1024]{2,1,0:T(8,128)(2,1)} %t.1, ...), custom_call_target="tpu_custom_call" | custom-call | tf_op jit(solution)/shard_map/pipe/pallas_call | solution.py:250
  481.0 1.4 reduce_sum.9
  483.0 33.1 %psum.7 = f32[]{:T(128)} all-reduce(f32[]{:T(128)S(6)} %mul.3), channel_id=1, replica_groups=mesh['dp'=4,'pp'=4] {'dp','pp'}, use_global_device_ids=true, to_apply=%region_1.0 | all-reduce | flops 1 | bytes 8 | tf_op jit(solution)/shard_map/psum | solution.py:478
  516.1 577.5 %grads.1 = (f32[2,1024,4096]{2,1,0:T(8,128)}, f32[2,4096,1024]{2,1,0:T(8,128)}) custom-call(bf16[2,4096,1024]{2,1,0:T(8,128)(2,1)} %get-tuple-element.10.hl, bf16[2,4096,1024]{2,1,0:T(8,128)(2,1)} %get-tuple-element.11.gl, bf16[2,1024,4096]{2,1,0:T(8,128)(2,1)} %bitcast.5, bf16[2,4096,1024]{2,1,0:T(8,128)(2,1)} %bitcast.7, ...), custom_call_target="tpu_custom_call" | custom-call | tf_op jit(solution)/shard_map/grads/pallas_call | solution.py:445
  1093.7 0.0 slice-start
  1093.7 0.0 slice-start.1
  1093.7 0.0 slice-start.2
  1093.7 0.0 slice-start.3
  1093.7 0.0 slice-start.4
  1093.7 0.0 slice-start.5
  1093.7 0.0 slice-start.6
  1093.7 0.0 slice-start.7
  1093.7 26.7 %copy.9 = f32[1,2,1024,4096]{3,2,1,0:T(8,128)} copy(f32[1,2,1024,4096]{3,2,1,0:T(8,128)} %bitcast.11) | data formatting | bytes 67108864
  1120.4 0.0 slice-done
  1120.4 0.0 slice-done.1
  1120.4 0.0 slice-done.2
  1120.4 0.0 slice-done.3
  1120.4 1.5 slice-done.4
  1122.0 1.2 slice-done.5
  1123.2 1.2 slice-done.6
  1124.3 1.2 slice-done.7
  1125.5 11.7 %copy.10 = f32[1,2,4096,1024]{3,2,1,0:T(8,128)} copy(f32[1,2,4096,1024]{3,2,1,0:T(8,128)S(1)} %bitcast.10) | data formatting | bytes 67108864
  (1 shorter events, 0.0 us)
Async XLA Ops:
  1093.7 26.8 %slice-start = ((s8[33554432]{0:T(1024)(128)(4,1)}), s8[4194304]{0:T(1024)(128)(4,1)S(1)}, s32[]{:S(2)}) async-start(s8[33554432]{0:T(1024)(128)(4,1)} %bitcast.8), calls=%async_computation | async-start | bytes 8388608
  1093.7 26.8 %slice-start.1 = ((s8[33554432]{0:T(1024)(128)(4,1)}), s8[4194304]{0:T(1024)(128)(4,1)S(1)}, s32[]{:S(2)}) async-start(s8[33554432]{0:T(1024)(128)(4,1)} %bitcast.8), calls=%async_computation.1 | async-start | bytes 8388608
  1093.7 26.7 %slice-start.2 = ((s8[33554432]{0:T(1024)(128)(4,1)}), s8[4194304]{0:T(1024)(128)(4,1)S(1)}, s32[]{:S(2)}) async-start(s8[33554432]{0:T(1024)(128)(4,1)} %bitcast.8), calls=%async_computation.2 | async-start | bytes 8388608
  1093.7 26.7 %slice-start.3 = ((s8[33554432]{0:T(1024)(128)(4,1)}), s8[4194304]{0:T(1024)(128)(4,1)S(1)}, s32[]{:S(2)}) async-start(s8[33554432]{0:T(1024)(128)(4,1)} %bitcast.8), calls=%async_computation.3 | async-start | bytes 8388608
  1093.7 28.3 %slice-start.4 = ((s8[33554432]{0:T(1024)(128)(4,1)}), s8[4194304]{0:T(1024)(128)(4,1)S(1)}, s32[]{:S(2)}) async-start(s8[33554432]{0:T(1024)(128)(4,1)} %bitcast.8), calls=%async_computation.4 | async-start | bytes 8388608
  1093.7 29.4 %slice-start.5 = ((s8[33554432]{0:T(1024)(128)(4,1)}), s8[4194304]{0:T(1024)(128)(4,1)S(1)}, s32[]{:S(2)}) async-start(s8[33554432]{0:T(1024)(128)(4,1)} %bitcast.8), calls=%async_computation.5 | async-start | bytes 8388608
  1093.7 30.6 %slice-start.6 = ((s8[33554432]{0:T(1024)(128)(4,1)}), s8[4194304]{0:T(1024)(128)(4,1)S(1)}, s32[]{:S(2)}) async-start(s8[33554432]{0:T(1024)(128)(4,1)} %bitcast.8), calls=%async_computation.6 | async-start | bytes 8388608
  1093.7 31.8 %slice-start.7 = ((s8[33554432]{0:T(1024)(128)(4,1)}), s8[4194304]{0:T(1024)(128)(4,1)S(1)}, s32[]{:S(2)}) async-start(s8[33554432]{0:T(1024)(128)(4,1)} %bitcast.8), calls=%async_computation.7 | async-start | bytes 8388608

commit v2 on v0

v2 whole, which is shorter than its diff:
```python
import functools
import math

import jax
import jax.numpy as jnp
from jax import lax
from jax.experimental import pallas as pl
from jax.experimental.pallas import tpu as pltpu
from jax.sharding import PartitionSpec as P

MESH = pl.DeviceIdType.MESH
F32 = jnp.float32
BF16 = jnp.bfloat16
VMEM_LIMIT = 67_043_328
C0 = math.sqrt(2.0 / math.pi)
C1 = 0.044715

D = 1024
FF = 4096
R = 256
NK = 16
FC = 256
NF = FF // FC
ND = D // FC
LAG, TAIL = 2, 2
TOK = R * NK

BC = 256
NB = FF // BC
HB = BC // 2
NS = 2
TC = 1024
NQ = 2 * TOK // TC
SPG = TC // R

NT = (((1,), (1,)), ((), ()))


def _dot(a, b):
    return jnp.dot(a, b, preferred_element_type=F32)


def _dot_t(a, b):
    return lax.dot_general(a, b, NT, preferred_element_type=F32)


def _t(i):
    return slice(i * FC, (i + 1) * FC)


def _sum(parts):
    return functools.reduce(lambda a, b: a + b, parts)


def _act(u):
    t2 = u * u
    th = jnp.tanh(u * (C0 + (C0 * C1) * t2))
    return th, 0.5 * u, t2


def _gelu(u):
    th, hu, _ = _act(u)
    return hu + hu * th


def _dgelu(th, hu, t2):
    return (0.5 + 0.5 * th) + (hu * (1.0 - th * th)) * (C0 + (3.0 * C0 * C1) * t2)


def _chain(up, mid, down, lag, tail):
    acc = [None] * ND
    act = {}

    def add(f, n):
        part = down(f, n, act[f])
        acc[n] = part if acc[n] is None else acc[n] + part

    for f in range(NF + lag):
        if f < NF:
            act[f] = mid(f, up(f))
        if lag <= f < NF + lag - tail:
            for n in range(ND):
                add(f - lag, n)
    for n in range(ND):
        for f in range(NF - tail, NF):
            add(f, n)
    return acc


def _kernel(inv, x, t, w1, w2, o1, o2, oloss, hl, gl, wl1, wl2, us,
            W1, W2, hin, gin, hgb, r1, r2, lo, lt,
            sw, sx, sg, su, sh0, sg2, shg, sop, lh, lg, swl, rwl,
            sld, swb, sxs, sxr, ssl, sscw, ssccw, rab, rc, rd, sf, slt, rlt):
    e = lax.axis_index('dp')
    s = lax.axis_index('pp')
    c = s % 2
    xx = s // 2
    owner = e // 2
    tcore = 2 * xx + owner
    partner = 2 * xx + 1 - c
    first = s == 0
    last = s == 3


    def wcopy(j, i):
        if i == 0:
            return pltpu.make_async_copy(w1.at[j], W1.at[j], sw.at[2 * j])
        return pltpu.make_async_copy(w2.at[j], W2.at[j], sw.at[2 * j + 1])

    for j in range(2):
        for i in range(2):
            wcopy(j, i).start()

    def micro(arr, k):
        return arr.at[k // 2, pl.ds(pl.multiple_of((k % 2) * R, R), R)]

    def xcopy(k):
        return pltpu.make_async_copy(micro(x, k), hin.at[k], sx.at[k])

    def tcopy(k):
        return pltpu.make_async_copy(micro(t, k), gin.at[k], sg.at[k])

    @pl.when(first)
    def _():
        lax.fori_loop(0, NK, lambda k, z: (xcopy(k).start(), z)[1], 0)

    @pl.when(last)
    def _():
        lax.fori_loop(0, NK, lambda k, z: (tcopy(k).start(), z)[1], 0)

    def wl_copy(i):
        src, dst = ((w1, wl1), (w2, wl2))[i]
        return pltpu.make_async_remote_copy(src.at[e % 2], dst, swl.at[i], rwl.at[i],
                                            device_id=(e, partner), device_id_type=MESH)

    @pl.when(c == owner)
    def _():
        for i in range(2):
            wl_copy(i).start()

    lo[...] = jnp.zeros_like(lo)


    def rows(k):
        return pl.ds(pl.multiple_of(k * R, R), R)

    def ship(src, dst, k, j, sem, land):
        d = 2 * c + j

        @pl.when(d == e)
        def _():
            pltpu.make_async_copy(src, dst.at[e % 2, rows(k)], sem).start()

        @pl.when(d != e)
        def _():
            pltpu.make_async_remote_copy(src, dst.at[e % 2, rows(k)], sem, land.at[e % 2, k // SPG],
                                         device_id=(d, tcore), device_id_type=MESH).start()

    def tile_wait(buf, sem):
        pltpu.make_async_copy(buf, hl.at[0, pl.ds(0, R)], sem).wait()

    def pipeline(ub, hop):
        def store_wait(p, j):
            pltpu.make_async_copy(ub.at[p, j], us.at[j, 0], su.at[p, j]).wait()

        def fwd(k, z):
            h4 = k % 4
            h2 = k % 2
            pltpu.make_async_copy(hl.at[0, pl.ds(0, R)], hin.at[k], sx.at[k]).wait()

            @pl.when(k == 0)
            def _():
                for j in range(2):
                    wcopy(j, 0).wait()
                    wcopy(j, 1).wait()

            @pl.when(k >= 2)
            def _():
                store_wait(h2, 0)
                store_wait(h2, 1)

            @pl.when(k >= 4)
            def _():
                tile_wait(hgb.at[h4], shg.at[h4])

            @pl.when(jnp.logical_and(k >= 2, s < 3))
            def _():
                tile_wait(hop.at[h2], sop.at[h2])
            ship(hin.at[k], hl, k, 0, sh0, lh)

            def layer(h, j, dst):
                def up(f):
                    return _sum(_dot(h[i], W1[j, _t(i), _t(f)]) for i in range(ND))

                def mid(f, u):
                    u = u.astype(BF16)
                    ub[h2, j, :, _t(f)] = u
                    return _gelu(u.astype(F32)).astype(BF16)

                def down(f, n, a):
                    return _dot(a, W2[j, _t(f), _t(n)])

                out = []
                for n, v in enumerate(_chain(up, mid, down, LAG, TAIL)):
                    out.append((h[n].astype(F32) + v).astype(BF16))
                    dst[:, _t(n)] = out[n]
                return out

            h1 = layer([hin[k, :, _t(n)] for n in range(ND)], 0, hgb.at[h4])
            layer(h1, 1, hop.at[h2])

            @pl.when(s < 3)
            def _():
                pltpu.make_async_remote_copy(hop.at[h2], hin.at[k], sop.at[h2], sx.at[k],
                                             device_id=(e, s + 1), device_id_type=MESH).start()
            for j in range(2):
                pltpu.make_async_copy(ub.at[h2, j], us.at[j, k], su.at[h2, j]).start()
            ship(hgb.at[h4], hl, k, 1, shg.at[h4], lh)

            @pl.when(last)
            def _():
                tcopy(k).wait()
                r = hop[h2].astype(F32) - gin[k].astype(F32)
                lo[...] += jnp.sum((r * r).reshape(R // 8, 8, D), axis=0)
                gin[k] = (r * inv).astype(BF16)
            return z

        lax.fori_loop(0, NK, fwd, 0)

        def uload(k, j):
            return pltpu.make_async_copy(us.at[j, k], ub.at[k % 2, j], su.at[k % 2, j])

        for k in range(2):
            for j in range(2):
                store_wait(k, j)
                uload(k, j).start()

        def bwd(k, z):
            h4 = k % 4
            h2 = k % 2

            @pl.when(s < 3)
            def _():
                pltpu.make_async_copy(hl.at[0, pl.ds(0, R)], gin.at[k], sg.at[k]).wait()
            uload(k, 0).wait()
            uload(k, 1).wait()
            tile_wait(hgb.at[h4], shg.at[h4])

            @pl.when(jnp.where(s == 0, k < 2, jnp.logical_or(k >= 2, s < 3)))
            def _():
                tile_wait(hop.at[h2], sop.at[h2])
            ship(gin.at[k], gl, k, 1, sg2, lg)

            def layer(g, j, dst):
                def up(f):
                    return _sum(_dot_t(g[i], W2[j, _t(f), _t(i)]) for i in range(ND))

                def mid(f, q):
                    th, hu, t2 = _act(ub[h2, j, :, _t(f)].astype(F32))
                    return (_dgelu(th, hu, t2) * q).astype(BF16)

                def down(f, n, ee):
                    return _dot_t(ee, W1[j, _t(n), _t(f)])

                out = []
                for n, v in enumerate(_chain(up, mid, down, LAG, TAIL)):
                    out.append((g[n].astype(F32) + v).astype(BF16))
                    dst[:, _t(n)] = out[n]
                return out

            def g2():
                return [gin[k, :, _t(n)] for n in range(ND)]

            @pl.when(s == 0)
            def _():
                layer(g2(), 1, hgb.at[h4])

            @pl.when(s > 0)
            def _():
                layer(layer(g2(), 1, hgb.at[h4]), 0, hop.at[h2])
                pltpu.make_async_remote_copy(hop.at[h2], gin.at[k], sop.at[h2], sg.at[k],
                                             device_id=(e, s - 1), device_id_type=MESH).start()
            ship(hgb.at[h4], gl, k, 0, shg.at[h4], lg)

            @pl.when(k < NK - 2)
            def _():
                uload(k + 2, 0).start()
                uload(k + 2, 1).start()
            return z

        lax.fori_loop(0, NK, bwd, 0)

        @pl.when(s > 0)
        def _():
            for i in range(2):
                tile_wait(hop.at[i], sop.at[i])

    pl.run_scoped(pipeline, pltpu.VMEM((2, 2, R, FF), BF16), pltpu.VMEM((2, R, D), BF16))


    jj = e % 2
    zz = e // 2
    yy = e % 2
    nxt = 2 * yy + 1 - zz
    prv = 2 * (1 - yy) + zz

    def shipped(j):
        if j == 0:
            pltpu.make_async_copy(hl.at[0], gl.at[0], sh0).wait()
            for i in range(4):
                tile_wait(hgb.at[i], shg.at[i])
        else:
            pltpu.make_async_copy(hl.at[0], gl.at[0], sg2).wait()

    for j in range(2):
        @pl.when(2 * c + j == e)
        def _():
            shipped(j)

    @pl.when(c != owner)
    def _():
        for i in range(2):
            wl_copy(i).wait_recv()

    @pl.when(last)
    def _():
        v = lo[:, :128]
        for i in range(1, D // 128):
            v = v + lo[:, i * 128:(i + 1) * 128]
        lt[e] = v

    def loss_copy(i):
        to = (4 * e + s + i) % 16
        return pltpu.make_async_remote_copy(lt.at[e], lt.at[e], slt.at[i], rlt.at[e],
                                            device_id=(to // 4, to % 4), device_id_type=MESH)

    def hview(q):
        return W2.at[q // 4, pl.ds(pl.multiple_of((q % 4) * TC, TC), TC), :]

    def gview(q):
        return W1.at[q // 4, :, pl.ds(pl.multiple_of((q % 4) * D, D), D)]

    def landed(q):
        sl = q % 2

        @pl.when(2 * c + sl != e)
        def _():
            part = hl.at[0, pl.ds(0, TC)]
            pltpu.make_async_copy(part, part, lh.at[sl, q // 2]).wait()
            pltpu.make_async_copy(part, part, lg.at[sl, q // 2]).wait()

    def load(q):
        src = (q % 2, pl.ds(pl.multiple_of((q // 2) * TC, TC), TC))
        return (pltpu.make_async_copy(hl.at[src], hview(q), sld.at[0, q]),
                pltpu.make_async_copy(gl.at[src], gview(q), sld.at[1, q]))

    def region(i, j, b, half):
        cs = pl.ds(pl.multiple_of(b * BC + half * HB, HB), HB)
        return o1.at[j, :, cs] if i == 0 else o2.at[j, cs, :]

    def grads(wb1, wb2, wt, p1, p2, f1, f2):
        def wload_start(b):
            sl = b % 2
            cs = pl.ds(pl.multiple_of(b * BC, BC), BC)

            @pl.when(c == owner)
            def _():
                pltpu.make_async_copy(w1.at[jj, :, cs], wb1.at[sl], swb.at[sl, 0]).start()
                pltpu.make_async_copy(w2.at[jj, cs, :], wb2.at[sl], swb.at[sl, 1]).start()

            @pl.when(c != owner)
            def _():
                pltpu.make_async_copy(wl1.at[:, cs], wb1.at[sl], swb.at[sl, 0]).start()
                pltpu.make_async_copy(wl2.at[cs, :], wb2.at[sl], swb.at[sl, 1]).start()

        def wload_wait(b):
            sl = b % 2
            pltpu.make_async_copy(wl1.at[:, pl.ds(0, BC)], wb1.at[sl], swb.at[sl, 0]).wait()
            pltpu.make_async_copy(wl2.at[pl.ds(0, BC), :], wb2.at[sl], swb.at[sl, 1]).wait()

        def start_load(q):
            landed(q)
            for cp in load(q):
                cp.start()

        wload_start(0)
        start_load(0)

        mine = pl.ds(pl.multiple_of(c * HB, HB), HB)
        theirs = pl.ds(pl.multiple_of((1 - c) * HB, HB), HB)

        def exchange(b):
            sl = b % 2
            return [pltpu.make_async_remote_copy(p.at[sl, theirs, :], r.at[sl], sxs.at[sl, i], sxr.at[sl, i],
                                                 device_id=(e, partner), device_id_type=MESH)
                    for i, (p, r) in enumerate(((p1, r1), (p2, r2)))]

        def sent(b):
            for i, f in enumerate((f1, f2)):
                for sem in (sscw, ssccw, ssl):
                    pltpu.make_async_copy(f.at[b % NS], region(i, 0, 0, 0), sem.at[i, b % NS]).wait()

        def finish(b):
            sl = b % 2
            fs = b % NS
            for cp in exchange(b):
                cp.wait()

            @pl.when(b >= NS)
            def _():
                sent(b)
            f1[fs] = (p1[sl, mine, :] + r1[sl]).T
            f2[fs] = p2[sl, mine, :] + r2[sl]
            for i, f in enumerate((f1, f2)):
                dst = region(i, jj, b, c)
                pltpu.make_async_remote_copy(f.at[fs], dst, sscw.at[i, fs], rab.at[c, i, b],
                                             device_id=(nxt, tcore), device_id_type=MESH).start()
                pltpu.make_async_remote_copy(f.at[fs], dst, ssccw.at[i, fs], rab.at[1 - c, i, b],
                                             device_id=(prv, tcore), device_id_type=MESH).start()

                @pl.when(c == owner)
                def _():
                    pltpu.make_async_copy(f.at[fs], dst, ssl.at[i, fs]).start()

                @pl.when(c != owner)
                def _():
                    pltpu.make_async_remote_copy(f.at[fs], dst, ssl.at[i, fs], rd.at[i],
                                                 device_id=(e, tcore), device_id_type=MESH).start()

        def block(b, z):
            sl = b % 2
            wload_wait(b)
            wt[...] = wb1[sl].T
            p1[sl] = jnp.zeros((BC, D), F32)
            p2[sl] = jnp.zeros((BC, D), F32)

            @pl.when(b < NB - 1)
            def _():
                wload_start(b + 1)

            def chunk(q, z2):
                @pl.when(b == 0)
                def _():
                    @pl.when(q < NQ - 3)
                    def _():
                        start_load(q + 1)
                    for cp in load(q):
                        cp.wait()

                hq = hview(q)
                gq = gview(q)
                es, acts = [], []
                for i in range(TC // FC):
                    ut = _dot_t(wt[...], hq[_t(i), :])
                    qt = _dot_t(wb2[sl], gq[_t(i), :])
                    th, hu, t2 = _act(ut.astype(BF16).astype(F32))
                    acts.append((hu + hu * th).astype(BF16))
                    es.append((_dgelu(th, hu, t2) * qt).astype(BF16))
                for n in range(ND):
                    p1[sl, :, _t(n)] += _sum(_dot(es[i], hq[_t(i), _t(n)]) for i in range(TC // FC))
                    p2[sl, :, _t(n)] += _sum(_dot(acts[i], gq[_t(i), _t(n)]) for i in range(TC // FC))

                @pl.when(jnp.logical_and(b == 0, q == NQ - 3))
                def _():
                    start_load(NQ - 2)
                    start_load(NQ - 1)

                @pl.when(jnp.logical_and(q == 0, b > 0))
                def _():
                    finish(b - 1)
                return z2

            lax.fori_loop(0, NQ, chunk, 0)
            for cp in exchange(b):
                cp.start()
            return z

        lax.fori_loop(0, 1, block, 0)

        @pl.when(last)
        def _():
            for i in range(1, 16):
                loss_copy(i).start()

        lax.fori_loop(1, NB, block, 0)
        finish(NB - 1)
        for b in range(NB - NS, NB):
            sent(b)

    pl.run_scoped(grads, pltpu.VMEM((2, D, BC), BF16), pltpu.VMEM((2, BC, D), BF16), pltpu.VMEM((BC, D), BF16),
                  pltpu.VMEM((2, BC, D), F32), pltpu.VMEM((2, BC, D), F32),
                  pltpu.VMEM((NS, D, HB), F32), pltpu.VMEM((NS, HB, D), F32))

    cw = prv // 2 == c
    src_chip = jnp.where(cw, prv, nxt)
    half = jnp.where(cw, 0, 1)
    onward = jnp.where(cw, nxt, prv)

    def forward(b, z):
        for i in range(2):
            reg = region(i, src_chip % 2, b, half)
            pltpu.make_async_remote_copy(reg, reg, sf.at[i], rab.at[0, i, b],
                                         device_id=(onward, s), device_id_type=MESH).wait_recv()
            pltpu.make_async_remote_copy(reg, reg, sf.at[i], rc.at[half, i],
                                         device_id=(onward, s), device_id_type=MESH).start()
        return z

    lax.fori_loop(0, NB, forward, 0)

    def others(b, z):
        for i in range(2):
            reg = region(i, src_chip % 2, b, 1 - half)
            pltpu.make_async_remote_copy(reg, reg, sf.at[i], rab.at[1, i, b],
                                         device_id=(onward, s), device_id_type=MESH).wait_recv()
        return z

    lax.fori_loop(0, NB, others, 0)


    for i in range(2):
        big = o1.at[0, :, pl.ds(0, FF // 2)] if i == 0 else o2.at[0, pl.ds(0, FF // 2), :]
        pltpu.make_async_copy(big, big, sf.at[i]).wait()

        @pl.when(c == owner)
        def _():
            pltpu.make_async_copy(big, big, rd.at[i]).wait()

        @pl.when(c != owner)
        def _():
            pltpu.make_async_copy(big, big, rc.at[0, i]).wait()
            pltpu.make_async_copy(big, big, rc.at[1, i]).wait()

    for j in range(2):
        @pl.when(2 * c + j != e)
        def _():
            shipped(j)

    @pl.when(c == owner)
    def _():
        for i in range(2):
            wl_copy(i).wait_send()

    @pl.when(last)
    def _():
        for i in range(1, 16):
            loss_copy(i).wait_send()

    for i in range(4):
        @pl.when(jnp.logical_not(jnp.logical_and(last, e == i)))
        def _():
            pltpu.make_async_remote_copy(lt.at[i], lt.at[i], slt.at[0], rlt.at[i],
                                         device_id=(e, s), device_id_type=MESH).wait_recv()
    oloss[0, 0] = jnp.sum((lt[0] + lt[1]) + (lt[2] + lt[3])) * (0.5 * inv)


def _call(x, t, w1, w2, inv):
    hbm = pl.BlockSpec(memory_space=pl.ANY)
    dma = pltpu.SemaphoreType.DMA
    vmem = pltpu.VMEM
    out = pl.pallas_call(
        functools.partial(_kernel, inv),
        name="train_step",
        out_shape=(
            jax.ShapeDtypeStruct((2, D, FF), F32),
            jax.ShapeDtypeStruct((2, FF, D), F32),
            jax.ShapeDtypeStruct((1, 1), F32),
            jax.ShapeDtypeStruct((2, TOK, D), BF16),
            jax.ShapeDtypeStruct((2, TOK, D), BF16),
            jax.ShapeDtypeStruct((D, FF), BF16),
            jax.ShapeDtypeStruct((FF, D), BF16),
            jax.ShapeDtypeStruct((2, NK, R, FF), BF16),
        ),
        in_specs=[hbm] * 4,
        out_specs=(hbm, hbm, pl.BlockSpec(memory_space=pltpu.SMEM)) + (hbm,) * 5,
        scratch_shapes=[
            vmem((2, D, FF), BF16), vmem((2, FF, D), BF16),
            vmem((NK, R, D), BF16), vmem((NK, R, D), BF16), vmem((4, R, D), BF16),
            vmem((2, HB, D), F32), vmem((2, HB, D), F32),
            vmem((8, D), F32), vmem((4, 8, 128), F32),
            dma((4,)), dma((NK,)), dma((NK,)), dma((2, 2)), dma, dma,
            dma((4,)), dma((2,)), dma((2, NK // SPG)), dma((2, NK // SPG)), dma((2,)), dma((2,)),
            dma((2, NQ)), dma((2, 2)), dma((2, 2)), dma((2, 2)),
            dma((2, NS)), dma((2, NS)), dma((2, NS)), dma((2, 2, NB)), dma((2, 2)), dma((2,)), dma((2,)),
            dma((16,)), dma((4,)),
        ],
        compiler_params=pltpu.CompilerParams(has_side_effects=True, vmem_limit_bytes=VMEM_LIMIT),
    )(x, t, w1, w2)
    return out[:3]


def solution(mesh):
    ndp = mesh.shape['dp']

    def body(x, t, w1, w2):
        nm, tok, d = x.shape
        dw1, dw2, loss = _call(x, t, w1[0], w2[0], 1.0 / (nm * tok * ndp * d))
        return dw1[None], dw2[None], loss[0, 0]

    return jax.shard_map(body, mesh=mesh,
                         in_specs=(P(None, 'dp', None), P(None, 'dp', None), P('pp'), P('pp')),
                         out_specs=(P('pp'), P('pp'), P()), check_vma=False)
```

time: 3280 us -> 1050 us (0.32)
  matrix products: 1580 us -> 0 us
  waiting for transfers between devices: 1080 us -> 0 us
  Pallas kernels: 0 us -> 1010 us
  local copies, waits for them, and re-layouts: 266 us -> 43.5 us
  starting transfers between devices: 147 us -> 0 us
  other arithmetic: 96.7 us -> 0.01 us
  blocking collectives: 52.7 us -> 0 us
    dot_general x132 -> x0, matrix products: 1580 us -> none  [the longest x22 335 us: bwd_step(): dw1 = dw1.at[j].add(jnp.dot(h.T, e, preferred_element_type=jnp.float32))]
    psum x1 -> x0, waiting for transfers between devices: 1080 us -> none  [body(): dw1 = lax.psum(dw1, 'dp')]
    pallas_call x0 -> x1, Pallas kernels: none -> 1010 us  [_call(): pl.pallas_call(functools.partial(_kernel, inv), name='train_step', out_sh...]
    ppermute x22 -> x0, starting transfers between devices: 147 us -> none  [the longest x11 133 us: fwd_step(): recv = lax.ppermute(h, 'pp', down)]
    dynamic_slice x55 -> x0, local copies, waits for them, and re-layouts: 146 us -> none  [the longest x22 103 us: fwd_step(): ubuf = ubuf.at[j, mc].set(jnp.where(valid, u, ubuf[j, mc]))]
    broadcast_in_dim x5 -> x0, local copies, waits for them, and re-layouts: 54.5 us -> none  [the longest x1 21.2 us: body(): jnp.zeros((2, nm, tok, ff), jnp.bfloat16)]
    psum x1 -> x0, blocking collectives: 52.7 us -> none  [body(): loss = lax.psum(lsum * inv, ('dp', 'pp'))]
    scatter x11 -> x0, other arithmetic: 40 us -> none  [fwd_step(): hbuf = hbuf.at[j, mc].set(jnp.where(valid, h, hbuf[j, mc]))]
  transfers between devices with their start and end apart: 23 -> 0, of which waited for: 1 -> 0; matrix products, arithmetic and copies ran while one was open for 21% -> 0% of each run, Pallas kernels for 0% -> 0%
where the time goes in v2:
time: 1050 us
  Pallas kernels  1010 us (96%)
  local copies, waits for them, and re-layouts  43.5 us (4%)
    pallas_call x1, Pallas kernels, _call(): pl.pallas_call(functools.partial(_kernel, inv), name='train_step', out_sh...  1010 us
    unnamed x18, local copies, waits for them, and re-layouts  43.5 us

profile of v2, /device:TPU:0, one launch (start us, length us, event | category | flops | bytes accessed | tf_op | source)
XLA Modules:
  0.0 1053.5 jit_solution(2600501998949520327)
XLA Ops:
  0.6 1007.5 %train_step.1 = (f32[2,1024,4096]{2,1,0:T(8,128)}, f32[2,4096,1024]{2,1,0:T(8,128)}, f32[1,1]{1,0:T(1,128)}, bf16[2,4096,1024]{2,1,0:T(8,128)(2,1)}, bf16[2,4096...) custom-call(bf16[8,512,1024]{2,1,0:T(8,128)(2,1)} %x.1, ...), custom_call_target="tpu_custom_call" | custom-call | tf_op jit(solution)/shard_map/train_step/pallas_call | solution.py:560
  1008.1 0.0 slice-start
  1008.1 0.0 slice-start.1
  1008.2 0.0 slice-start.2
  1008.2 0.0 slice-start.3
  1008.2 0.0 slice-start.4
  1008.2 0.0 slice-start.5
  1008.2 0.0 slice-start.6
  1008.2 0.0 slice-start.7
  1008.2 26.7 %copy.10 = f32[1,2,1024,4096]{3,2,1,0:T(8,128)} copy(f32[1,2,1024,4096]{3,2,1,0:T(8,128)} %bitcast.8) | data formatting | bytes 67108864
  1034.9 0.0 slice-done
  1034.9 0.0 slice-done.1
  1034.9 0.0 slice-done.2
  1034.9 0.0 slice-done.3
  1034.9 1.5 slice-done.4
  1036.4 1.2 slice-done.5
  1037.6 1.2 slice-done.6
  1038.8 1.2 slice-done.7
  1040.0 11.7 %copy.11 = f32[1,2,4096,1024]{3,2,1,0:T(8,128)} copy(f32[1,2,4096,1024]{3,2,1,0:T(8,128)S(1)} %bitcast.7) | data formatting | bytes 67108864
  (1 shorter events, 0.0 us)
Async XLA Ops:
  1008.1 26.8 %slice-start = ((s8[33554432]{0:T(1024)(128)(4,1)}), s8[4194304]{0:T(1024)(128)(4,1)S(1)}, s32[]{:S(2)}) async-start(s8[33554432]{0:T(1024)(128)(4,1)} %bitcast.5), calls=%async_computation | async-start | bytes 8388608
  1008.1 26.8 %slice-start.1 = ((s8[33554432]{0:T(1024)(128)(4,1)}), s8[4194304]{0:T(1024)(128)(4,1)S(1)}, s32[]{:S(2)}) async-start(s8[33554432]{0:T(1024)(128)(4,1)} %bitcast.5), calls=%async_computation.1 | async-start | bytes 8388608
  1008.2 26.7 %slice-start.2 = ((s8[33554432]{0:T(1024)(128)(4,1)}), s8[4194304]{0:T(1024)(128)(4,1)S(1)}, s32[]{:S(2)}) async-start(s8[33554432]{0:T(1024)(128)(4,1)} %bitcast.5), calls=%async_computation.2 | async-start | bytes 8388608
  1008.2 26.7 %slice-start.3 = ((s8[33554432]{0:T(1024)(128)(4,1)}), s8[4194304]{0:T(1024)(128)(4,1)S(1)}, s32[]{:S(2)}) async-start(s8[33554432]{0:T(1024)(128)(4,1)} %bitcast.5), calls=%async_computation.3 | async-start | bytes 8388608
  1008.2 28.3 %slice-start.4 = ((s8[33554432]{0:T(1024)(128)(4,1)}), s8[4194304]{0:T(1024)(128)(4,1)S(1)}, s32[]{:S(2)}) async-start(s8[33554432]{0:T(1024)(128)(4,1)} %bitcast.5), calls=%async_computation.4 | async-start | bytes 8388608
  1008.2 29.4 %slice-start.5 = ((s8[33554432]{0:T(1024)(128)(4,1)}), s8[4194304]{0:T(1024)(128)(4,1)S(1)}, s32[]{:S(2)}) async-start(s8[33554432]{0:T(1024)(128)(4,1)} %bitcast.5), calls=%async_computation.5 | async-start | bytes 8388608
  1008.2 30.6 %slice-start.6 = ((s8[33554432]{0:T(1024)(128)(4,1)}), s8[4194304]{0:T(1024)(128)(4,1)S(1)}, s32[]{:S(2)}) async-start(s8[33554432]{0:T(1024)(128)(4,1)} %bitcast.5), calls=%async_computation.6 | async-start | bytes 8388608
  1008.2 31.8 %slice-start.7 = ((s8[33554432]{0:T(1024)(128)(4,1)}), s8[4194304]{0:T(1024)(128)(4,1)S(1)}, s32[]{:S(2)}) async-start(s8[33554432]{0:T(1024)(128)(4,1)} %bitcast.5), calls=%async_computation.7 | async-start | bytes 8388608
